TPU v7x, 32 devices: a whole 2x2x4 slice. The times are simulated.
32 devices in a mesh: leaf: 4 (over y, core), grid: 8 (over z, x).
Axes of the slice: x: 2, y: 2, z: 4, core: 2. Of those that a mesh axis runs over, the one named last changes fastest.
Arguments:
- ainv_sep: bfloat16 [4, 2048, 2048], P('leaf', 'grid'), may hold values from -6 to 6
- l_panel: bfloat16 [4, 2048, 512], P('leaf', 'grid'), may hold values from -0.125 to 0.125
- block_mask: int32 [4, 1, 4], P('leaf'), may hold values 0 or 1
- owner: int32 [4, 4], P('leaf'), may hold values 0 or 1
- dinv: float32 [4, 512, 512], P('leaf', 'grid'), may hold values from -6 to 6
Outputs:
- ainv_panel: bfloat16 [4, 2048, 512], P('leaf', 'grid')
- ainv_upper: bfloat16 [4, 512, 2048], P('leaf', 'grid')
- ainv_diag: float32 [4, 512, 512], P('leaf', 'grid')
All inputs are finite; a program needn't handle non-finite values. No bound on the sum of `block_mask` or of `owner` on one device may be relied on, other than what follows from the above.
Results may differ from a plain program's by a relative error of at most 0.0019.
Values may be sent and summed in bfloat16 or wider, within the bound.
No kernel may reach another device: no remote copies, remote signals or barrier semaphores. Data moves between devices by JAX's collectives and lax.ppermute only.
A program may use at most 128 MiB of HBM per device.

v0:
```python
import jax
import jax.numpy as jnp
from jax import lax
from jax.sharding import PartitionSpec as P

B = 512


def swapped(array, axis, stride):
    return lax.ppermute(array, axis, [(i, i ^ 1 << stride) for i in range(lax.axis_size(axis))])


def body(ainv_sep, l_panel, block_mask, owner, dinv):
    strip_rows = ainv_sep.shape[1]
    block_count = block_mask.shape[2]
    sibling = swapped(ainv_sep, "leaf", 0)
    colmask = jnp.repeat(owner[0], B)
    mixed = jnp.where(colmask[None, :] == 1, sibling[0], ainv_sep[0])
    first_row = lax.axis_index("grid") * strip_rows
    row_block = (first_row + jnp.arange(strip_rows, dtype=jnp.int32)) // B
    onehot = (row_block[:, None] == jnp.arange(block_count, dtype=jnp.int32)[None, :]).astype(
        jnp.float32
    )
    row_flags = jnp.dot(
        onehot, block_mask[0].T.astype(jnp.float32), preferred_element_type=jnp.float32
    )
    flags_wide = jnp.repeat(row_flags, B, axis=1)
    masked = jnp.where(flags_wide > 0.5, l_panel[0], jnp.zeros((), jnp.bfloat16))
    whole_panel = lax.all_gather(masked, "grid", axis=0, tiled=True)
    panel = (-jnp.dot(mixed, whole_panel, preferred_element_type=jnp.float32)).astype(jnp.bfloat16)
    upper = lax.all_to_all(panel.T, "grid", split_axis=0, concat_axis=1, tiled=True)
    diag = dinv[0] - jnp.dot(upper, whole_panel, preferred_element_type=jnp.float32)
    return (panel[None], upper[None], diag[None])


def solution(mesh):
    placed = (
        P("leaf", "grid", None),
        P("leaf", "grid", None),
        P("leaf", None, None),
        P("leaf", None),
        P("leaf", "grid", None),
    )
    return jax.shard_map(
        body,
        mesh=mesh,
        in_specs=placed,
        out_specs=(P("leaf", "grid", None), P("leaf", "grid", None), P("leaf", "grid", None)),
        check_vma=False,
    )
```

profile of v0, /device:TPU:0, one launch (start us, length us, event | category | flops | bytes accessed | tf_op | source)
XLA Modules:
  0.0 85.9 jit_solution(1391319304822525056)
XLA Ops:
  7.2 0.0 all-gather.2.cloned.1.call-start
  7.2 0.9 %fusion.4 = f32[1,256]{1,0:T(1,128)S(1)} fusion(s32[256]{0:T(256)S(1)} %and_select_fusion, s32[1,1,4]{2,1,0:T(1,128)} %param.7), kind=kOutput, calls=%fused_computation.9 | convolution fusion | flops 3076 | bytes 2064 | tf_op jit(solution)/shard_map/dot_general | solution.py:24
  8.1 1.8 %bitcast_select_fusion.2 = bf16[256,512]{1,0:T(8,128)(2,1)} fusion(bf16[1,256,512]{2,1,0:T(8,128)(2,1)} %param.6, pred[256]{0:T(512)(128)(4,1)S(1)} %broadcast_compare_fusion), kind=kLoop, calls=%fused_computation.7 | loop fusion | flops 131072 | bytes 524544 | tf_op jit(solution)/shard_map/jit(_where)/select_n | solution.py:28
  9.9 0.0 all-gather.2.cloned.1.call-update
  9.9 0.6 collective-permute-start
  10.5 0.7 compare_bitcast_fusion
  11.1 0.1 broadcast_bitcast_fusion
  11.2 1.8 %collective-permute-done = bf16[1,256,2048]{2,1,0:T(8,128)(2,1)S(1)} collective-permute-done((bf16[1,256,2048]{2,1,0:T(8,128)(2,1)}, bf16[1,256,2048]{2,1,0:T(8,128)(2,1)S(1)}, u32[]{:S(2)}, u32[]{:S(2)}) %collective-permute-start) | collective-permute-done | bytes 1048608 | tf_op jit(solution)/shard_map/ppermute | solution.py:10
  13.0 49.6 %all-gather.2.cloned.1.call-done = bf16[2048,512]{1,0:T(8,128)(2,1)} async-done(((bf16[256,512]{1,0:T(8,128)(2,1)}), bf16[2048,512]{1,0:T(8,128)(2,1)}) %all-gather.2.cloned.1.call-update) | async-done | bytes 2097168 | tf_op jit(solution)/shard_map/all_gather | solution.py:29
  62.5 2.7 %fusion = bf16[256,512]{1,0:T(8,128)(2,1)S(1)} fusion(bf16[2048,512]{1,0:T(8,128)(2,1)} %all-gather.2.cloned.1.call-done, bf16[1,256,2048]{2,1,0:T(8,128)(2,1)} %param.5, bf16[1,256,2048]{2,1,0:T(8,128)(2,1)S(1)} %collective-permute-done, pred[2048]{0:T(1024)(128)(4,1)S(1)} %bitcast.40), kind=kOutput, calls=%fused_computation.1 | convolution fusion | flops 537657344 | bytes 4458496 | tf_op jit(solution)/shard_map/dot_general | solution.py:30
  65.2 0.0 copy-start.1
  65.2 0.0 copy-start
  65.2 0.0 copy-start.2
  65.2 0.1 copy.11
  65.4 11.6 %all_to_all.19 = bf16[8,64,256]{2,1,0:T(8,128)(2,1)S(1)} all-to-all(bf16[8,64,256]{2,1,0:T(8,128)(2,1)S(1)} %bitcast.37), channel_id=1, replica_groups=mesh['leaf'=4,'grid'=8] {'grid'}, dimensions={0} | all-to-all | bytes 524288 | tf_op jit(solution)/shard_map/all_to_all | solution.py:31
  76.9 0.1 copy.12
  77.1 0.8 broadcast_in_dim.31
  77.9 0.0 copy-done
  77.9 0.0 copy-done.2
  77.9 1.1 %fusion.1 = f32[1,64,512]{2,1,0:T(8,128)} fusion(bf16[64,2048]{1,0:T(8,128)(2,1)S(1)} %bitcast.36, bf16[2048,512]{1,0:T(8,128)(2,1)S(1)} %copy-done, f32[1,64,512]{2,1,0:T(8,128)S(1)} %copy-done.2), kind=kOutput, calls=%fused_computation.3 | convolution fusion | flops 134250496 | bytes 2621440 | tf_op jit(solution)/shard_map/dot_general | solution.py:32
  79.1 0.0 copy-done.1
  (4 shorter events, 0.0 us)
Async XLA Ops:
  7.2 55.3 %all-gather.2.cloned.1.call-start = ((), (), s32[]{:S(2)}) async-start(), calls=%async_computation.1 | async-start | bytes 2359296 | tf_op jit(solution)/shard_map/all_gather | solution.py:29
  9.9 3.1 %collective-permute-start = (bf16[1,256,2048]{2,1,0:T(8,128)(2,1)}, bf16[1,256,2048]{2,1,0:T(8,128)(2,1)S(1)}, u32[]{:S(2)}, u32[]{:S(2)}) collective-permute-start(bf16[1,256,2048]{2,1,0:T(8,128)(2,1)} %param.5), channel_id=1, source_target_pairs={{0,8},{8,0},{16,24},{24,16},{1,9},{9,1},{17,25},{25,17},{2,10},{10... | collective-permute-start | bytes 3145736 | tf_op jit(solution)/shard_map/ppermute | solution.py:10
  65.2 13.9 %copy-start.1 = (bf16[256,512]{1,0:T(8,128)(2,1)}, bf16[256,512]{1,0:T(8,128)(2,1)S(1)}, u32[]{:S(2)}) copy-start(bf16[256,512]{1,0:T(8,128)(2,1)S(1)} %fusion) | copy-start | bytes 786436
  65.2 12.7 %copy-start = (bf16[2048,512]{1,0:T(8,128)(2,1)S(1)}, bf16[2048,512]{1,0:T(8,128)(2,1)}, u32[]{:S(2)}) copy-start(bf16[2048,512]{1,0:T(8,128)(2,1)} %all-gather.2.cloned.1.call-done) | copy-start | bytes 6291460
  65.2 12.7 %copy-start.2 = (f32[1,64,512]{2,1,0:T(8,128)S(1)}, f32[1,64,512]{2,1,0:T(8,128)}, u32[]{:S(2)}) copy-start(f32[1,64,512]{2,1,0:T(8,128)} %param.9) | copy-start | bytes 393220
Sparse Core Ops, SparseCore 0:
  10.7 51.7 all-gather.1
where the time goes:
time: 86.2 us; the launch traced here: 85.9 us
  waiting for transfers between devices  51.3 us (60%)
  between operations  14.1 us (16%)
  blocking collectives  11.6 us (13%)
  matrix products  4.67 us (5%)
  other arithmetic  2.44 us (3%)
  local copies, waits for them, and re-layouts  1.23 us (1%)
    all_gather x1, waiting for transfers between devices, body(): whole_panel = lax.all_gather(masked, 'grid', axis=0, tiled=True)  49.6 us
    all_to_all x1, blocking collectives, body(): lax.all_to_all(panel.T, 'grid', split_axis=0, concat_axis=1, tiled=True)  11.6 us
    dot_general x1, matrix products, body(): jnp.dot(mixed, whole_panel, preferred_element_type=jnp.float32)  2.66 us
    select_n x1, other arithmetic, body(): jnp.where(flags_wide > 0.5, l_panel[0], jnp.zeros((), jnp.bfloat16))  1.76 us
    ppermute x1, waiting for transfers between devices, swapped(): lax.ppermute(array, axis, [(i, i ^ 1 << stride) for i in range(lax.axis_s...  1.75 us
  transfers between devices with their start and end apart: 2, of which 2 were waited for; matrix products, arithmetic and copies ran while one was open for 1% of the time, Pallas kernels for 0%

commit v1 on v0

--- a/solution.py
+++ b/solution.py
@@ -26,7 +26,12 @@
     )
     flags_wide = jnp.repeat(row_flags, B, axis=1)
     masked = jnp.where(flags_wide > 0.5, l_panel[0], jnp.zeros((), jnp.bfloat16))
-    whole_panel = lax.all_gather(masked, "grid", axis=0, tiled=True)
+    ring = [masked]
+    for hop in range(7):
+        ring.append(lax.ppermute(ring[-1], "grid", [(dev, (dev + 1) % 8) for dev in range(8)]))
+    whole_panel = jnp.roll(
+        jnp.concatenate(ring[::-1], axis=0), (lax.axis_index("grid") + 1) * ring[0].shape[0], axis=0
+    )
     panel = (-jnp.dot(mixed, whole_panel, preferred_element_type=jnp.float32)).astype(jnp.bfloat16)
     upper = lax.all_to_all(panel.T, "grid", split_axis=0, concat_axis=1, tiled=True)
     diag = dinv[0] - jnp.dot(upper, whole_panel, preferred_element_type=jnp.float32)

time: 86.2 us -> 89.5 us (1.038)
  waiting for transfers between devices: 51.3 us -> 64.9 us
  between operations: 14.1 us -> 0.86 us
  starting transfers between devices: 0.6 us -> 3.04 us
  local copies, waits for them, and re-layouts: 1.23 us -> 3.44 us
  blocking collectives: 11.6 us -> 10.6 us
    ppermute x0 -> x7, waiting for transfers between devices: none -> 64.9 us  [body(): lax.ppermute(ring[-1], 'grid', [(dev, (dev + 1) % 8) for dev in range(8)])]
    all_gather x1 -> x0, waiting for transfers between devices: 49.6 us -> none  [body(): whole_panel = lax.all_gather(masked, 'grid', axis=0, tiled=True)]
    ppermute x0 -> x7, starting transfers between devices: none -> 3.04 us  [body(): lax.ppermute(ring[-1], 'grid', [(dev, (dev + 1) % 8) for dev in range(8)])]
    unnamed x8 -> x26, local copies, waits for them, and re-layouts: 0.1 us -> 2.31 us
    dot_general x1, matrix products: 2.66 us -> 0.74 us  [body(): jnp.dot(mixed, whole_panel, preferred_element_type=jnp.float32)]
    ppermute x1, waiting for transfers between devices: 1.75 us -> 0.01 us  [swapped(): lax.ppermute(array, axis, [(i, i ^ 1 << stride) for i in range(lax.axis_s...]
    dot_general x1, matrix products: 1.13 us -> 2.72 us  [body(): jnp.dot(upper, whole_panel, preferred_element_type=jnp.float32)]
    all_to_all x1, blocking collectives: 11.6 us -> 10.6 us  [body(): lax.all_to_all(panel.T, 'grid', split_axis=0, concat_axis=1, tiled=True)]
  transfers between devices with their start and end apart: 2 -> 8, of which waited for: 2 -> 7; matrix products, arithmetic and copies ran while one was open for 1% -> 1% of each run, Pallas kernels for 0% -> 0%
where the time goes in v1:
time: 89.5 us; the launch traced here: 89.2 us
  waiting for transfers between devices  64.9 us (73%)
  blocking collectives  10.6 us (12%)
  matrix products  4.37 us (5%)
  local copies, waits for them, and re-layouts  3.44 us (4%)
  starting transfers between devices  3.04 us (3%)
  other arithmetic  1.96 us (2%)
    ppermute x7, waiting for transfers between devices, body(): lax.ppermute(ring[-1], 'grid', [(dev, (dev + 1) % 8) for dev in range(8)])  64.9 us
    all_to_all x1, blocking collectives, body(): lax.all_to_all(panel.T, 'grid', split_axis=0, concat_axis=1, tiled=True)  10.6 us
    ppermute x7, starting transfers between devices, body(): lax.ppermute(ring[-1], 'grid', [(dev, (dev + 1) % 8) for dev in range(8)])  3.04 us
    dot_general x1, matrix products, body(): jnp.dot(upper, whole_panel, preferred_element_type=jnp.float32)  2.72 us
    unnamed x26, local copies, waits for them, and re-layouts  2.31 us
  transfers between devices with their start and end apart: 8, of which 7 were waited for; matrix products, arithmetic and copies ran while one was open for 1% of the time, Pallas kernels for 0%

profile of v1, /device:TPU:0, one launch (start us, length us, event | category | flops | bytes accessed | tf_op | source)
XLA Modules:
  0.0 89.2 jit_solution(5227503015086629828)
XLA Ops:
  0.6 0.0 copy-start
  0.7 0.9 %fusion.18 = f32[1,256]{1,0:T(1,128)S(1)} fusion(s32[256]{0:T(256)S(1)} %and_select_fusion, s32[1,1,4]{2,1,0:T(1,128)} %param.7), kind=kOutput, calls=%fused_computation.13 | convolution fusion | flops 3076 | bytes 2064 | tf_op jit(solution)/shard_map/dot_general | solution.py:24
  1.6 1.1 %bitcast_select_fusion.2 = bf16[256,512]{1,0:T(8,128)(2,1)S(1)} fusion(bf16[1,256,512]{2,1,0:T(8,128)(2,1)} %param.6, pred[256]{0:T(512)(128)(4,1)S(1)} %broadcast_compare_fusion), kind=kLoop, calls=%fused_computation.11 | loop fusion | flops 131072 | bytes 524544 | tf_op jit(solution)/shard_map/jit(_where)/select_n | solution.py:28
  2.6 3.0 %collective-permute-start.1 = (bf16[256,512]{1,0:T(8,128)(2,1)S(1)}, bf16[256,512]{1,0:T(8,128)(2,1)S(1)}, u32[]{:S(2)}, u32[]{:S(2)}) collective-permute-start(bf16[256,512]{1,0:T(8,128)(2,1)S(1)} %bitcast_select_fusion.2), channel_id=1, source_target_pairs={{0,1},{1,2},{2,3},{3,4},{4,5},{5,6},{6,7},{7,0},{8,9},{9,10},{10,1... | collective-permute-start | bytes 786440 | tf_op jit(solution)/shard_map/ppermute | solution.py:31
  5.7 9.3 %collective-permute-done.1 = bf16[256,512]{1,0:T(8,128)(2,1)S(1)} collective-permute-done((bf16[256,512]{1,0:T(8,128)(2,1)S(1)}, bf16[256,512]{1,0:T(8,128)(2,1)S(1)}, u32[]{:S(2)}, u32[]{:S(2)}) %collective-permute-start.1) | collective-permute-done | bytes 262176 | tf_op jit(solution)/shard_map/ppermute | solution.py:31
  15.0 0.0 collective-permute-start.2
  15.0 10.2 %collective-permute-done.2 = bf16[256,512]{1,0:T(8,128)(2,1)S(1)} collective-permute-done((bf16[256,512]{1,0:T(8,128)(2,1)S(1)}, bf16[256,512]{1,0:T(8,128)(2,1)S(1)}, u32[]{:S(2)}, u32[]{:S(2)}) %collective-permute-start.2) | collective-permute-done | bytes 262176 | tf_op jit(solution)/shard_map/ppermute | solution.py:31
  25.2 0.0 collective-permute-start.3
  25.2 9.3 %collective-permute-done.3 = bf16[256,512]{1,0:T(8,128)(2,1)S(1)} collective-permute-done((bf16[256,512]{1,0:T(8,128)(2,1)S(1)}, bf16[256,512]{1,0:T(8,128)(2,1)S(1)}, u32[]{:S(2)}, u32[]{:S(2)}) %collective-permute-start.3) | collective-permute-done | bytes 262176 | tf_op jit(solution)/shard_map/ppermute | solution.py:31
  34.5 0.0 collective-permute-start.4
  34.5 9.1 %collective-permute-done.4 = bf16[256,512]{1,0:T(8,128)(2,1)S(1)} collective-permute-done((bf16[256,512]{1,0:T(8,128)(2,1)S(1)}, bf16[256,512]{1,0:T(8,128)(2,1)S(1)}, u32[]{:S(2)}, u32[]{:S(2)}) %collective-permute-start.4) | collective-permute-done | bytes 262176 | tf_op jit(solution)/shard_map/ppermute | solution.py:31
  43.6 0.0 collective-permute-start.5
  43.6 9.1 %collective-permute-done.5 = bf16[256,512]{1,0:T(8,128)(2,1)S(1)} collective-permute-done((bf16[256,512]{1,0:T(8,128)(2,1)S(1)}, bf16[256,512]{1,0:T(8,128)(2,1)S(1)}, u32[]{:S(2)}, u32[]{:S(2)}) %collective-permute-start.5) | collective-permute-done | bytes 262176 | tf_op jit(solution)/shard_map/ppermute | solution.py:31
  52.6 0.0 collective-permute-start.6
  52.6 0.0 collective-permute-start
  52.6 9.7 %collective-permute-done.6 = bf16[256,512]{1,0:T(8,128)(2,1)S(1)} collective-permute-done((bf16[256,512]{1,0:T(8,128)(2,1)S(1)}, bf16[256,512]{1,0:T(8,128)(2,1)S(1)}, u32[]{:S(2)}, u32[]{:S(2)}) %collective-permute-start.6) | collective-permute-done | bytes 262176 | tf_op jit(solution)/shard_map/ppermute | solution.py:31
  62.3 0.0 collective-permute-start.7
  62.3 0.7 compare_bitcast_fusion
  63.0 0.1 broadcast_bitcast_fusion
  63.1 0.0 copy-start.4
  63.1 8.3 %collective-permute-done.7 = bf16[256,512]{1,0:T(8,128)(2,1)S(1)} collective-permute-done((bf16[256,512]{1,0:T(8,128)(2,1)S(1)}, bf16[256,512]{1,0:T(8,128)(2,1)S(1)}, u32[]{:S(2)}, u32[]{:S(2)}) %collective-permute-start.7) | collective-permute-done | bytes 262176 | tf_op jit(solution)/shard_map/ppermute | solution.py:31
  71.6 0.0 copy-done
  71.6 0.1 constant_dynamic-update-slice_fusion.8
  71.9 0.0 copy-start.3
  71.9 0.1 constant_dynamic-update-slice_fusion
  72.0 0.0 copy-start.1
  72.0 0.0 collective-permute-done
  72.0 1.9 %copy-done.1 = bf16[4096,512]{1,0:T(8,128)(2,1)} copy-done((bf16[4096,512]{1,0:T(8,128)(2,1)}, bf16[4096,512]{1,0:T(8,128)(2,1)S(1)}, u32[]{:S(2)}) %copy-start.1) | copy-done | bytes 4194328
  74.0 0.0 copy-done.4
  74.0 0.7 fusion.7
  74.7 0.0 copy-start.2
  74.7 0.1 copy.11
  74.9 10.6 %all_to_all.19 = bf16[8,64,256]{2,1,0:T(8,128)(2,1)S(1)} all-to-all(bf16[8,64,256]{2,1,0:T(8,128)(2,1)S(1)} %bitcast.38), channel_id=1, replica_groups=mesh['leaf'=4,'grid'=8] {'grid'}, dimensions={0} | all-to-all | bytes 524288 | tf_op jit(solution)/shard_map/all_to_all | solution.py:36
  85.5 0.2 copy.12
  85.7 0.8 broadcast_in_dim.31
  86.5 0.0 copy-done.3
  86.5 2.7 %fusion.13 = f32[1,64,512]{2,1,0:T(8,128)} fusion(bf16[64,2048]{1,0:T(8,128)(2,1)S(1)} %bitcast.39, bf16[4096,512]{1,0:T(8,128)(2,1)} %copy-done.1, s32[]{:T(128)S(6)} %select_n.34, f32[1,64,512]{2,1,0:T(8,128)S(1)} %copy-done.3), kind=kOutput, calls=%fused_computation.7 | convolution fusion | flops 134250496 | bytes 2621444 | tf_op jit(solution)/shard_map/dot_general | solution.py:37
  89.2 0.0 copy-done.2
  (18 shorter events, 0.3 us)
Async XLA Ops:
  0.6 70.9 %copy-start = (bf16[1,256,512]{2,1,0:T(8,128)(2,1)S(1)}, bf16[1,256,512]{2,1,0:T(8,128)(2,1)}, u32[]{:S(2)}) copy-start(bf16[1,256,512]{2,1,0:T(8,128)(2,1)} %param.6) | copy-start | bytes 786436
  2.6 12.4 %collective-permute-start.1 = (bf16[256,512]{1,0:T(8,128)(2,1)S(1)}, bf16[256,512]{1,0:T(8,128)(2,1)S(1)}, u32[]{:S(2)}, u32[]{:S(2)}) collective-permute-start(bf16[256,512]{1,0:T(8,128)(2,1)S(1)} %bitcast_select_fusion.2), channel_id=1, source_target_pairs={{0,1},{1,2},{2,3},{3,4},{4,5},{5,6},{6,7},{7,0},{8,9},{9,10},{10,1... | collective-permute-start | bytes 786440 | tf_op jit(solution)/shard_map/ppermute | solution.py:31
  15.0 10.2 %collective-permute-start.2 = (bf16[256,512]{1,0:T(8,128)(2,1)S(1)}, bf16[256,512]{1,0:T(8,128)(2,1)S(1)}, u32[]{:S(2)}, u32[]{:S(2)}) collective-permute-start(bf16[256,512]{1,0:T(8,128)(2,1)S(1)} %collective-permute-done.1), channel_id=1, source_target_pairs={{0,1},{1,2},{2,3},{3,4},{4,5},{5,6},{6,7},{7,0},{8,9},{9,10},{10,1... | collective-permute-start | bytes 786440 | tf_op jit(solution)/shard_map/ppermute | solution.py:31
  25.2 9.3 %collective-permute-start.3 = (bf16[256,512]{1,0:T(8,128)(2,1)S(1)}, bf16[256,512]{1,0:T(8,128)(2,1)S(1)}, u32[]{:S(2)}, u32[]{:S(2)}) collective-permute-start(bf16[256,512]{1,0:T(8,128)(2,1)S(1)} %collective-permute-done.2), channel_id=1, source_target_pairs={{0,1},{1,2},{2,3},{3,4},{4,5},{5,6},{6,7},{7,0},{8,9},{9,10},{10,1... | collective-permute-start | bytes 786440 | tf_op jit(solution)/shard_map/ppermute | solution.py:31
  34.5 9.1 %collective-permute-start.4 = (bf16[256,512]{1,0:T(8,128)(2,1)S(1)}, bf16[256,512]{1,0:T(8,128)(2,1)S(1)}, u32[]{:S(2)}, u32[]{:S(2)}) collective-permute-start(bf16[256,512]{1,0:T(8,128)(2,1)S(1)} %collective-permute-done.3), channel_id=1, source_target_pairs={{0,1},{1,2},{2,3},{3,4},{4,5},{5,6},{6,7},{7,0},{8,9},{9,10},{10,1... | collective-permute-start | bytes 786440 | tf_op jit(solution)/shard_map/ppermute | solution.py:31
  43.6 9.1 %collective-permute-start.5 = (bf16[256,512]{1,0:T(8,128)(2,1)S(1)}, bf16[256,512]{1,0:T(8,128)(2,1)S(1)}, u32[]{:S(2)}, u32[]{:S(2)}) collective-permute-start(bf16[256,512]{1,0:T(8,128)(2,1)S(1)} %collective-permute-done.4), channel_id=1, source_target_pairs={{0,1},{1,2},{2,3},{3,4},{4,5},{5,6},{6,7},{7,0},{8,9},{9,10},{10,1... | collective-permute-start | bytes 786440 | tf_op jit(solution)/shard_map/ppermute | solution.py:31
  52.6 9.7 %collective-permute-start.6 = (bf16[256,512]{1,0:T(8,128)(2,1)S(1)}, bf16[256,512]{1,0:T(8,128)(2,1)S(1)}, u32[]{:S(2)}, u32[]{:S(2)}) collective-permute-start(bf16[256,512]{1,0:T(8,128)(2,1)S(1)} %collective-permute-done.5), channel_id=1, source_target_pairs={{0,1},{1,2},{2,3},{3,4},{4,5},{5,6},{6,7},{7,0},{8,9},{9,10},{10,1... | collective-permute-start | bytes 786440 | tf_op jit(solution)/shard_map/ppermute | solution.py:31
  52.6 19.4 %collective-permute-start = (bf16[1,256,2048]{2,1,0:T(8,128)(2,1)}, bf16[1,256,2048]{2,1,0:T(8,128)(2,1)S(1)}, u32[]{:S(2)}, u32[]{:S(2)}) collective-permute-start(bf16[1,256,2048]{2,1,0:T(8,128)(2,1)} %param.5), channel_id=1, source_target_pairs={{0,8},{8,0},{16,24},{24,16},{1,9},{9,1},{17,25},{25,17},{2,10},{10... | collective-permute-start | bytes 3145736 | tf_op jit(solution)/shard_map/ppermute | solution.py:10
  62.3 9.1 %collective-permute-start.7 = (bf16[256,512]{1,0:T(8,128)(2,1)S(1)}, bf16[256,512]{1,0:T(8,128)(2,1)S(1)}, u32[]{:S(2)}, u32[]{:S(2)}) collective-permute-start(bf16[256,512]{1,0:T(8,128)(2,1)S(1)} %collective-permute-done.6), channel_id=1, source_target_pairs={{0,1},{1,2},{2,3},{3,4},{4,5},{5,6},{6,7},{7,0},{8,9},{9,10},{10,1... | collective-permute-start | bytes 786440 | tf_op jit(solution)/shard_map/ppermute | solution.py:31
  63.1 10.9 %copy-start.4 = (bf16[1,256,2048]{2,1,0:T(8,128)(2,1)S(1)}, bf16[1,256,2048]{2,1,0:T(8,128)(2,1)}, u32[]{:S(2)}) copy-start(bf16[1,256,2048]{2,1,0:T(8,128)(2,1)} %param.5) | copy-start | bytes 3145732
  71.9 14.6 %copy-start.3 = (f32[1,64,512]{2,1,0:T(8,128)S(1)}, f32[1,64,512]{2,1,0:T(8,128)}, u32[]{:S(2)}) copy-start(f32[1,64,512]{2,1,0:T(8,128)} %param.9) | copy-start | bytes 393220
  72.0 2.0 %copy-start.1 = (bf16[4096,512]{1,0:T(8,128)(2,1)}, bf16[4096,512]{1,0:T(8,128)(2,1)S(1)}, u32[]{:S(2)}) copy-start(bf16[4096,512]{1,0:T(8,128)(2,1)S(1)} %constant_dynamic-update-slice_fusion) | copy-start | bytes 12582916
  74.7 14.5 %copy-start.2 = (bf16[256,512]{1,0:T(8,128)(2,1)}, bf16[256,512]{1,0:T(8,128)(2,1)S(1)}, u32[]{:S(2)}) copy-start(bf16[256,512]{1,0:T(8,128)(2,1)S(1)} %fusion.7) | copy-start | bytes 786436
